TPU v7x, 256 devices: a whole 4x4x8 slice. The times are simulated.
256 devices in a mesh: section: 2 (over x_hi), feat: 16 (over y, x_lo, core), width: 8 (over z).
Axes of the slice: x: 4 (x_hi: 2, x_lo: 2; x = x_hi * 2 + x_lo), y: 4, z: 8, core: 2. Of those that a mesh axis runs over, the one named last changes fastest.
Arguments:
- mlp_inputs: bfloat16 [4, 1024, 2304], P('section', 'width'), may hold values from -6 to 6
- encoder: bfloat16 [4, 2304, 16384], P('section', 'width', 'feat'), may hold values from -0.125 to 0.125
- enc_bias: float32 [4, 16384], P('section', 'feat'), may hold values from -3 to 3
- decoder: bfloat16 [10, 16384, 2304], P('section', 'feat', 'width'), may hold values from -0.046875 to 0.046875
- dec_bias: float32 [4, 2304], P(None, 'width'), may hold values from -3 to 3
- targets: bfloat16 [4, 1024, 2304], P(None, None, 'width'), may hold values from -6 to 6
- live_rows: int32 [1024], replicated, may hold values 0 or 1
Outputs:
- errors: bfloat16 [4, 1024, 2304], P(None, None, 'width')
- gradients: bfloat16 [10, 16384, 2304], P('section', 'feat', 'width')
All inputs are finite; a program needn't handle non-finite values.
Results may differ from a plain program's by a relative error of at most 0.0042.
Values may be sent and summed in bfloat16 or wider, within the bound.
No kernel may reach another device: no remote copies, remote signals or barrier semaphores. Data moves between devices by JAX's collectives and lax.ppermute only.
A program may use at most 128 MiB of HBM per device.

v0:
```python
import jax
import jax.numpy as jnp
from jax import lax
from jax.sharding import PartitionSpec as P


def from_behind(value, axis, steps):
    count = lax.axis_size(axis)
    initial, last = (max(0, -steps), min(count, count - steps))
    return lax.ppermute(value, axis, [(source, source + steps) for source in range(initial, last)])


def pair_tables(layer_count):
    source_ids = []
    target_ids = []
    for source in range(layer_count):
        for target in range(source, layer_count):
            source_ids.append(source)
            target_ids.append(target)
    return (jnp.array(source_ids, jnp.int32), jnp.array(target_ids, jnp.int32))


def local(mlp_inputs, encoder, enc_bias, decoder, dec_bias, targets, live_rows):
    layers_here, tok_local, model_width = mlp_inputs.shape
    pre_act = jnp.einsum(
        "ltd,ldf->tlf",
        mlp_inputs,
        lax.all_gather(encoder, "width", axis=1, tiled=True),
        preferred_element_type=jnp.float32,
    )
    local_feats = jnp.maximum(pre_act + enc_bias[None, :, :], 0.0).astype(jnp.bfloat16)
    token_feats = lax.all_gather(local_feats, "width", axis=0, tiled=True)
    layers_all = dec_bias.shape[0]
    tokens_all = live_rows.shape[0]
    per_section = decoder.shape[0]
    source_ids, target_ids = pair_tables(layers_all)
    section_id = lax.axis_index("section")
    earlier = from_behind(token_feats[:, layers_here - 1], "section", 1)
    features = jnp.concatenate([earlier[:, None, :], token_feats], axis=1)
    first_layer = section_id * layers_here - 1
    rebuilt = jnp.zeros((layers_all, tokens_all, decoder.shape[2]), jnp.float32)
    chosen = []
    for pair_slot in range(per_section):
        pair_id = section_id * per_section + pair_slot
        source = source_ids[pair_id]
        target = target_ids[pair_id]
        picked = lax.dynamic_index_in_dim(features, source - first_layer, 1, keepdims=False)
        chosen.append((picked, target))
        partial_value = jnp.dot(picked, decoder[pair_slot], preferred_element_type=jnp.float32)
        current = lax.dynamic_index_in_dim(rebuilt, target, 0, keepdims=False)
        rebuilt = lax.dynamic_update_index_in_dim(rebuilt, current + partial_value, target, 0)
    summed = lax.psum(rebuilt, ("section", "feat"))
    keep_rows = live_rows.astype(jnp.float32)[None, :, None]
    errors = ((summed + dec_bias[:, None, :] - targets.astype(jnp.float32)) * keep_rows).astype(
        jnp.bfloat16
    )
    gradients = []
    for picked, target in chosen:
        residual = lax.dynamic_index_in_dim(errors, target, 0, keepdims=False)
        product = lax.dot_general(
            picked, residual, (((0,), (0,)), ((), ())), preferred_element_type=jnp.float32
        )
        gradients.append((product / tokens_all).astype(jnp.bfloat16))
    return (errors, jnp.stack(gradients))


def solution(mesh):
    placed = (
        P("section", "width", None),
        P("section", "width", "feat"),
        P("section", "feat"),
        P("section", "feat", "width"),
        P(None, "width"),
        P(None, None, "width"),
        P(),
    )
    return jax.shard_map(
        local,
        mesh=mesh,
        in_specs=placed,
        out_specs=(P(None, None, "width"), P("section", "feat", "width")),
        check_vma=False,
    )
```

profile of v0, /device:TPU:1, one launch (start us, length us, event | category | flops | bytes accessed | tf_op | source)
XLA Modules:
  0.0 397.8 jit_solution(8431505922366384273)
XLA Ops:
  7.2 0.0 copy-start
  7.2 0.0 all-gather.3.cloned.1.call-start
  7.2 0.7 all-gather.3.cloned.1.call-update
  7.9 0.0 all-gather.5.cloned.1.call-start
  8.0 109.4 %all-gather.3.cloned.1.call-done = bf16[2,2304,1024]{2,1,0:T(8,128)(2,1)} async-done(((bf16[2,288,1024]{2,1,0:T(8,128)(2,1)}), bf16[2,2304,1024]{2,1,0:T(8,128)(2,1)}) %all-gather.3.cloned.1.call-update) | async-done | bytes 9437200 | tf_op jit(solution)/shard_map/all_gather | solution.py:28
  117.3 0.0 copy-done
  117.3 7.3 %fusion.36 = bf16[128,2,1024]{0,2,1:T(8,128)(2,1)} fusion(bf16[2,2304,1024]{2,1,0:T(8,128)(2,1)} %all-gather.3.cloned.1.call-done, bf16[2,128,2304]{2,1,0:T(8,128)(2,1)S(1)} %copy-done, f32[2,1024]{1,0:T(2,128)} %param.11), kind=kOutput, calls=%fused_computation.59 | convolution fusion | flops 1208745984 | bytes 11149312 | tf_op jit(solution)/shard_map/ltd,ldf->tlf/dot_general | solution.py:25
  124.7 0.0 copy-start.5
  124.7 0.0 copy-start.6
  124.7 0.0 all-gather.5.cloned.1.call-update
  124.7 0.0 all-reduce.2.cloned.1.call-start
  124.7 57.6 %all-gather.5.cloned.1.call-done = bf16[1024,2,1024]{0,2,1:T(8,128)(2,1)} async-done(((bf16[128,2,1024]{0,2,1:T(8,128)(2,1)}), bf16[1024,2,1024]{0,2,1:T(8,128)(2,1)}) %all-gather.5.cloned.1.call-update) | async-done | bytes 4194320 | tf_op jit(solution)/shard_map/all_gather | solution.py:32
  182.4 3.1 slice_bitcast_fusion
  185.4 4.4 %collective-permute-start = (bf16[1024,1024]{0,1:T(8,128)(2,1)}, bf16[1024,1024]{0,1:T(8,128)(2,1)S(1)}, u32[]{:S(2)}, u32[]{:S(2)}) collective-permute-start(bf16[1024,1024]{0,1:T(8,128)(2,1)} %slice_bitcast_fusion), channel_id=1, source_target_pairs={{0,128},{1,129},{2,130},{3,131},{4,132},{5,133},{6,134},{7,135},{8... | collective-permute-start | bytes 6291464 | tf_op jit(solution)/shard_map/ppermute | solution.py:10
  189.9 0.0 copy-done.5
  189.9 0.0 copy-done.6
  189.9 0.7 fusion.72
  203.2 26.7 %collective-permute-done = bf16[1024,1024]{0,1:T(8,128)(2,1)S(1)} collective-permute-done((bf16[1024,1024]{0,1:T(8,128)(2,1)}, bf16[1024,1024]{0,1:T(8,128)(2,1)S(1)}, u32[]{:S(2)}, u32[]{:S(2)}) %collective-permute-start) | collective-permute-done | bytes 2097184 | tf_op jit(solution)/shard_map/ppermute | solution.py:10
  229.9 0.0 copy-start.1
  229.9 3.0 broadcast_in_dim.25
  232.9 0.8 copy-done.1
  233.7 0.0 copy-start.3
  233.7 3.4 fusion.18
  237.1 1.3 constant_dynamic-slice_fusion.3
  238.5 0.0 copy-done.3
  238.5 2.2 fusion.17
  240.7 1.3 constant_dynamic-slice_fusion.2
  242.1 2.2 fusion.15
  244.3 1.3 constant_dynamic-slice_fusion.1
  245.6 2.3 fusion.13
  247.9 1.3 constant_dynamic-slice_fusion
  249.3 2.2 fusion.11
  251.5 0.0 copy-start.8
  251.5 0.0 copy-start.7
  251.5 0.0 all-reduce.2.cloned.1.call-update
  251.5 0.7 copy-done.8
  252.2 126.4 %all-reduce.2.cloned.1.call-done = f32[4,1024,288]{1,2,0:T(8,128)} async-done(((f32[4,1024,288]{1,2,0:T(8,128)}), f32[4,1024,288]{1,2,0:T(8,128)}) %all-reduce.2.cloned.1.call-update) | async-done | bytes 4718608 | tf_op jit(solution)/shard_map/psum | solution.py:52
  378.6 0.0 copy-done.7
  378.6 0.0 copy-start.2
  378.6 3.9 multiply_convert_fusion
  382.5 0.3 copy-done.2
  382.8 0.0 copy-start.4
  382.8 1.4 fusion.35
  384.2 1.4 fusion.33
  385.6 1.4 fusion.31
  386.9 1.4 fusion.29
  388.3 0.0 copy-done.4
  388.3 1.4 fusion.27
  389.7 0.0 copy-start.9
  389.7 1.6 copy-done.9
  (1 shorter events, 0.0 us)
Async XLA Ops:
  7.2 110.2 %copy-start = (bf16[2,128,2304]{2,1,0:T(8,128)(2,1)S(1)}, bf16[2,128,2304]{2,1,0:T(8,128)(2,1)}, u32[]{:S(2)}) copy-start(bf16[2,128,2304]{2,1,0:T(8,128)(2,1)} %param.9) | copy-start | bytes 3538948
  7.2 110.2 %all-gather.3.cloned.1.call-start = ((), (), s32[]{:S(2)}) async-start(), calls=%async_computation | async-start | bytes 10616832 | tf_op jit(solution)/shard_map/all_gather | solution.py:28
  7.9 174.4 %all-gather.5.cloned.1.call-start = ((), (), s32[]{:S(2)}) async-start(), calls=%async_computation.1 | async-start | bytes 4718592 | tf_op jit(solution)/shard_map/all_gather | solution.py:32
  124.7 65.2 %copy-start.5 = (s32[10]{0:T(128)S(1)}, s32[10]{0:T(128)}, u32[]{:S(2)}) copy-start(s32[10]{0:T(128)} %constant.92.clone) | copy-start | bytes 124
  124.7 65.2 %copy-start.6 = (s32[10]{0:T(128)S(1)}, s32[10]{0:T(128)}, u32[]{:S(2)}) copy-start(s32[10]{0:T(128)} %constant.93.clone) | copy-start | bytes 124
  124.7 253.9 %all-reduce.2.cloned.1.call-start = ((), (), s32[]{:S(2)}) async-start(), calls=%async_computation.2 | async-start | bytes 9437184 | tf_op jit(solution)/shard_map/psum | solution.py:52
  185.4 44.5 %collective-permute-start = (bf16[1024,1024]{0,1:T(8,128)(2,1)}, bf16[1024,1024]{0,1:T(8,128)(2,1)S(1)}, u32[]{:S(2)}, u32[]{:S(2)}) collective-permute-start(bf16[1024,1024]{0,1:T(8,128)(2,1)} %slice_bitcast_fusion), channel_id=1, source_target_pairs={{0,128},{1,129},{2,130},{3,131},{4,132},{5,133},{6,134},{7,135},{8... | collective-permute-start | bytes 6291464 | tf_op jit(solution)/shard_map/ppermute | solution.py:10
  229.9 3.8 copy-start.1
  233.7 4.7 %copy-start.3 = (bf16[5,1024,288]{1,2,0:T(8,128)(2,1)S(1)}, bf16[5,1024,288]{1,2,0:T(8,128)(2,1)}, u32[]{:S(2)}) copy-start(bf16[5,1024,288]{1,2,0:T(8,128)(2,1)} %param.12) | copy-start | bytes 8847364
  251.5 0.7 copy-start.8
  251.5 127.1 %copy-start.7 = (f32[4,288]{1,0:T(4,128)S(1)}, f32[4,288]{1,0:T(4,128)}, u32[]{:S(2)}) copy-start(f32[4,288]{1,0:T(4,128)} %param.13) | copy-start | bytes 13828
  378.6 4.2 %copy-start.2 = (bf16[1024,2,1024]{0,2,1:T(8,128)(2,1)S(1)}, bf16[1024,2,1024]{0,2,1:T(8,128)(2,1)}, u32[]{:S(2)}) copy-start(bf16[1024,2,1024]{0,2,1:T(8,128)(2,1)} %all-gather.5.cloned.1.call-done) | copy-start | bytes 12582916
  382.8 5.5 %copy-start.4 = (bf16[4,1024,288]{1,2,0:T(8,128)(2,1)}, bf16[4,1024,288]{1,2,0:T(8,128)(2,1)S(1)}, u32[]{:S(2)}) copy-start(bf16[4,1024,288]{1,2,0:T(8,128)(2,1)S(1)} %multiply_convert_fusion) | copy-start | bytes 7077892
  389.7 1.6 copy-start.9
Sparse Core Ops, SparseCore 0:
  9.8 107.5 all-gather.2
  124.8 57.5 all-gather.4
  251.6 126.9 all-reduce.1
where the time goes:
time: 398 us
  waiting for transfers between devices  321 us (81%)
  matrix products  26.5 us (7%)
  between operations  26.5 us (7%)
  local copies, waits for them, and re-layouts  15.5 us (4%)
  starting transfers between devices  4.52 us (1%)
    psum x1, waiting for transfers between devices, local(): summed = lax.psum(rebuilt, ('section', 'feat'))  126 us
    all_gather x1, waiting for transfers between devices, local(): lax.all_gather(encoder, 'width', axis=1, tiled=True)  109 us
    all_gather x1, waiting for transfers between devices, local(): token_feats = lax.all_gather(local_feats, 'width', axis=0, tiled=True)  57.6 us
    ppermute x1, waiting for transfers between devices, from_behind(): lax.ppermute(value, axis, [(source, source + steps) for source in range(i...  26.7 us
    dot_general x5, matrix products, local(): jnp.dot(picked, decoder[pair_slot], preferred_element_type=jnp.float32)  12.3 us
  transfers between devices with their start and end apart: 4, of which 4 were waited for; matrix products, arithmetic and copies ran while one was open for 0% of the time, Pallas kernels for 0%

commit v1 on v0

--- a/solution.py
+++ b/solution.py
@@ -2,6 +2,11 @@
 import jax.numpy as jnp
 from jax import lax
 from jax.sharding import PartitionSpec as P
+
+
+def exchange_gather(x, mesh_axis, dim):
+    sent = jnp.stack([x] * lax.axis_size(mesh_axis))
+    return jnp.concatenate(lax.all_to_all(sent, mesh_axis, 0, 0), axis=dim)
 
 
 def from_behind(value, axis, steps):
@@ -25,7 +30,7 @@
     pre_act = jnp.einsum(
         "ltd,ldf->tlf",
         mlp_inputs,
-        lax.all_gather(encoder, "width", axis=1, tiled=True),
+        exchange_gather(encoder, "width", 1),
         preferred_element_type=jnp.float32,
     )
     local_feats = jnp.maximum(pre_act + enc_bias[None, :, :], 0.0).astype(jnp.bfloat16)

time: 398 us -> 515 us (1.29)
  blocking collectives: 0 us -> 216 us
  waiting for transfers between devices: 321 us -> 210 us
  local copies, waits for them, and re-layouts: 15.5 us -> 27 us
    all_to_all x0 -> x1, blocking collectives: none -> 216 us  [exchange_gather(): return jnp.concatenate(lax.all_to_all(sent, mesh_axis, 0, 0), axis=dim)]
    all_gather x1 -> x0, waiting for transfers between devices: 109 us -> none  [local(): lax.all_gather(encoder, 'width', axis=1, tiled=True)]
    all_to_all x0 -> x1, local copies, waits for them, and re-layouts: none -> 8.87 us  [exchange_gather(): return jnp.concatenate(lax.all_to_all(sent, mesh_axis, 0, 0), axis=dim)]
  transfers between devices with their start and end apart: 4 -> 3, of which waited for: 4 -> 3; matrix products, arithmetic and copies ran while one was open for 0% -> 0% of each run, Pallas kernels for 0% -> 0%
where the time goes in v1:
time: 515 us
  blocking collectives  216 us (42%)
  waiting for transfers between devices  210 us (41%)
  local copies, waits for them, and re-layouts  27 us (5%)
  between operations  26.6 us (5%)
  matrix products  26.5 us (5%)
    all_to_all x1, blocking collectives, exchange_gather(): return jnp.concatenate(lax.all_to_all(sent, mesh_axis, 0, 0), axis=dim)  216 us
    psum x1, waiting for transfers between devices, local(): summed = lax.psum(rebuilt, ('section', 'feat'))  126 us
    all_gather x1, waiting for transfers between devices, local(): token_feats = lax.all_gather(local_feats, 'width', axis=0, tiled=True)  56.9 us
    ppermute x1, waiting for transfers between devices, from_behind(): lax.ppermute(value, axis, [(source, source + steps) for source in range(i...  26.9 us
    dot_general x5, matrix products, local(): jnp.dot(picked, decoder[pair_slot], preferred_element_type=jnp.float32)  12.4 us
  transfers between devices with their start and end apart: 3, of which 3 were waited for; matrix products, arithmetic and copies ran while one was open for 0% of the time, Pallas kernels for 0%

profile of v1, /device:TPU:1, one launch (start us, length us, event | category | flops | bytes accessed | tf_op | source)
XLA Modules:
  0.0 514.6 jit_solution(520107911801203818)
XLA Ops:
  7.2 0.0 copy-start
  7.2 0.0 all-gather.2.cloned.1.call-start
  7.2 2.6 stack.14
  9.8 216.0 %all_to_all.5 = bf16[8,2,288,1024]{3,2,1,0:T(8,128)(2,1)} all-to-all(bf16[8,2,288,1024]{3,2,1,0:T(8,128)(2,1)S(1)} %stack.14), channel_id=1, replica_groups=mesh['section'=2,'feat'=16,'width'=8] {'width'}, dimensions={0} | all-to-all | bytes 18874368 | tf_op jit(solution)/shard_map/all_to_all | solution.py:9
  225.8 0.0 copy-start.5
  225.8 8.9 %copy.13 = bf16[8,2,288,1024]{3,2,0,1:T(8,128)(2,1)} copy(bf16[8,2,288,1024]{3,2,1,0:T(8,128)(2,1)} %all_to_all.5) | data formatting | bytes 18874368 | tf_op jit(solution)/shard_map/all_to_all | solution.py:9
  234.7 0.0 copy-done
  234.7 0.0 copy-done.5
  234.7 7.3 %fusion.36 = bf16[128,2,1024]{0,2,1:T(8,128)(2,1)} fusion(bf16[2,2304,1024]{2,1,0:T(8,128)(2,1)} %bitcast.128, bf16[2,128,2304]{2,1,0:T(8,128)(2,1)S(1)} %copy-done, f32[2,1024]{1,0:T(2,128)S(1)} %copy-done.5), kind=kOutput, calls=%fused_computation.59 | convolution fusion | flops 1208745984 | bytes 11149312 | tf_op jit(solution)/shard_map/ltd,ldf->tlf/dot_general | solution.py:30
  242.0 0.0 copy-start.6
  242.0 0.0 copy-start.7
  242.0 0.0 all-gather.2.cloned.1.call-update
  242.0 0.0 all-reduce.2.cloned.1.call-start
  242.1 56.9 %all-gather.2.cloned.1.call-done = bf16[1024,2,1024]{0,2,1:T(8,128)(2,1)} async-done(((bf16[128,2,1024]{0,2,1:T(8,128)(2,1)}), bf16[1024,2,1024]{0,2,1:T(8,128)(2,1)}) %all-gather.2.cloned.1.call-update) | async-done | bytes 4194320 | tf_op jit(solution)/shard_map/all_gather | solution.py:37
  298.9 3.1 slice_bitcast_fusion
  302.0 4.4 collective-permute-start
  306.4 0.0 copy-done.6
  306.5 0.0 copy-done.7
  306.5 0.7 fusion.72
  319.6 26.9 %collective-permute-done = bf16[1024,1024]{0,1:T(8,128)(2,1)S(1)} collective-permute-done((bf16[1024,1024]{0,1:T(8,128)(2,1)}, bf16[1024,1024]{0,1:T(8,128)(2,1)S(1)}, u32[]{:S(2)}, u32[]{:S(2)}) %collective-permute-start) | collective-permute-done | bytes 2097184 | tf_op jit(solution)/shard_map/ppermute | solution.py:15
  346.5 0.0 copy-start.1
  346.5 3.0 broadcast_in_dim.25
  349.5 0.8 copy-done.1
  350.3 0.0 copy-start.3
  350.3 3.4 fusion.18
  353.7 1.3 constant_dynamic-slice_fusion.3
  355.1 0.0 copy-done.3
  355.1 2.2 fusion.17
  357.3 1.3 constant_dynamic-slice_fusion.2
  358.7 2.2 fusion.15
  360.9 1.3 constant_dynamic-slice_fusion.1
  362.2 2.3 fusion.13
  364.5 1.3 constant_dynamic-slice_fusion
  365.9 2.2 fusion.11
  368.1 0.0 copy-start.9
  368.1 0.0 copy-start.8
  368.1 0.0 all-reduce.2.cloned.1.call-update
  368.1 0.7 copy-done.9
  368.8 126.3 %all-reduce.2.cloned.1.call-done = f32[4,1024,288]{1,2,0:T(8,128)} async-done(((f32[4,1024,288]{1,2,0:T(8,128)}), f32[4,1024,288]{1,2,0:T(8,128)}) %all-reduce.2.cloned.1.call-update) | async-done | bytes 4718608 | tf_op jit(solution)/shard_map/psum | solution.py:57
  495.1 0.0 copy-done.8
  495.1 0.0 copy-start.2
  495.1 3.9 multiply_convert_fusion
  499.0 0.3 copy-done.2
  499.3 0.0 copy-start.4
  499.3 1.4 fusion.35
  500.7 1.4 fusion.33
  502.1 1.4 fusion.31
  503.4 1.4 fusion.29
  504.8 0.0 copy-done.4
  504.8 1.4 fusion.27
  506.2 0.0 copy-start.10
  506.2 1.6 copy-done.10
  (1 shorter events, 0.0 us)
Async XLA Ops:
  7.2 227.5 %copy-start = (bf16[2,128,2304]{2,1,0:T(8,128)(2,1)S(1)}, bf16[2,128,2304]{2,1,0:T(8,128)(2,1)}, u32[]{:S(2)}) copy-start(bf16[2,128,2304]{2,1,0:T(8,128)(2,1)} %param.9) | copy-start | bytes 3538948
  7.2 291.8 %all-gather.2.cloned.1.call-start = ((), (), s32[]{:S(2)}) async-start(), calls=%async_computation.1 | async-start | bytes 4718592 | tf_op jit(solution)/shard_map/all_gather | solution.py:37
  225.8 8.9 %copy-start.5 = (f32[2,1024]{1,0:T(2,128)S(1)}, f32[2,1024]{1,0:T(2,128)}, u32[]{:S(2)}) copy-start(f32[2,1024]{1,0:T(2,128)} %param.11) | copy-start | bytes 24580
  242.0 64.4 %copy-start.6 = (s32[10]{0:T(128)S(1)}, s32[10]{0:T(128)}, u32[]{:S(2)}) copy-start(s32[10]{0:T(128)} %constant.92.clone) | copy-start | bytes 124
  242.0 64.4 %copy-start.7 = (s32[10]{0:T(128)S(1)}, s32[10]{0:T(128)}, u32[]{:S(2)}) copy-start(s32[10]{0:T(128)} %constant.93.clone) | copy-start | bytes 124
  242.0 253.0 %all-reduce.2.cloned.1.call-start = ((), (), s32[]{:S(2)}) async-start(), calls=%async_computation.2 | async-start | bytes 9437184 | tf_op jit(solution)/shard_map/psum | solution.py:57
  302.0 44.5 %collective-permute-start = (bf16[1024,1024]{0,1:T(8,128)(2,1)}, bf16[1024,1024]{0,1:T(8,128)(2,1)S(1)}, u32[]{:S(2)}, u32[]{:S(2)}) collective-permute-start(bf16[1024,1024]{0,1:T(8,128)(2,1)} %slice_bitcast_fusion), channel_id=1, source_target_pairs={{0,128},{1,129},{2,130},{3,131},{4,132},{5,133},{6,134},{7,135},{8... | collective-permute-start | bytes 6291464 | tf_op jit(solution)/shard_map/ppermute | solution.py:15
  346.5 3.8 copy-start.1
  350.3 4.7 copy-start.3
  368.1 0.7 copy-start.9
  368.1 127.0 %copy-start.8 = (f32[4,288]{1,0:T(4,128)S(1)}, f32[4,288]{1,0:T(4,128)}, u32[]{:S(2)}) copy-start(f32[4,288]{1,0:T(4,128)} %param.13) | copy-start | bytes 13828
  495.1 4.2 copy-start.2
  499.3 5.5 %copy-start.4 = (bf16[4,1024,288]{1,2,0:T(8,128)(2,1)}, bf16[4,1024,288]{1,2,0:T(8,128)(2,1)S(1)}, u32[]{:S(2)}) copy-start(bf16[4,1024,288]{1,2,0:T(8,128)(2,1)S(1)} %multiply_convert_fusion) | copy-start | bytes 7077892
  506.2 1.6 copy-start.10
Sparse Core Ops, SparseCore 0:
  242.2 56.7 all-gather.1
  368.2 126.7 all-reduce.1
